TPU v7x, 32 devices: a whole 2x2x4 slice. The times are simulated.
32 devices in a mesh: gx: 2 (over y), gy: 4 (over z), gz: 4 (over x, core).
Axes of the slice: x: 2, y: 2, z: 4, core: 2. Of those that a mesh axis runs over, the one named last changes fastest.
Arguments:
- kinematics: float32 [18, 8192], P(None, ('gx', 'gy', 'gz')), may hold values from -6 to 6
- pair_offsets: float32 [3, 16, 8192], P(None, None, ('gx', 'gy', 'gz')), may hold values from -1 to 1
- pair_index: int32 [16, 8192], P(None, ('gx', 'gy', 'gz')), may hold values from 0 to 687, as said below
- neighbour_count: int32 [8192], P(('gx', 'gy', 'gz')), may hold values from 1 to 16
- send_rows: int32 [27, 512], P(None, ('gx', 'gy', 'gz')), may hold values from 0 to 255
- migrate_dir: int32 [8192], P(('gx', 'gy', 'gz')), may hold values from 0 to 26, as said below
- migrate_slot: int32 [8192], P(('gx', 'gy', 'gz')), may hold values from 0 to 3, as said below
- enc_node_w1: float32 [15, 128], replicated, may hold values from -1.5 to 1.5
- enc_node_w2: bfloat16 [128, 128], replicated, may hold values from -0.5 to 0.5
- enc_edge_w1: float32 [4, 128], replicated, may hold values from -3 to 3
- enc_edge_w2: bfloat16 [128, 128], replicated, may hold values from -0.5 to 0.5
- edge_w1: bfloat16 [3, 384, 128], replicated, may hold values from -0.3125 to 0.3125
- edge_w2: bfloat16 [3, 128, 128], replicated, may hold values from -0.5 to 0.5
- node_w1: bfloat16 [3, 256, 128], replicated, may hold values from -0.375 to 0.375
- node_w2: bfloat16 [3, 128, 128], replicated, may hold values from -0.5 to 0.5
- edge_gain: float32 [3, 128], replicated, may hold values from 0.25 to 1.75
- node_gain: float32 [3, 128], replicated, may hold values from 0.25 to 1.75
- dec_w1: bfloat16 [128, 128], replicated, may hold values from -0.5 to 0.5
- dec_w2: float32 [3, 128], replicated, may hold values from -0.5 to 0.5
Outputs:
- stayed: float32 [18, 8192], P(None, ('gx', 'gy', 'gz'))
- arrived: float32 [18, 3456], P(None, ('gx', 'gy', 'gz'))
Inputs may be any that keep to these rules, and one draw needn't show every extreme that they name: `pair_index`: A value below 256 names a row of the particle's own subdomain. A value v of 256 or more names ghost row v - 256; its direction (v - 256) // 16 is never 13 and points to a subdomain inside the grid. How many ghost rows of a direction are named differs between directions and subdomains. `migrate_dir`: A value other than 13 points to a subdomain inside the grid. On one subdomain at most 4 particles share a direction, and on every subdomain some direction has exactly 4. `migrate_slot`: among the particles of one subdomain that leave in one direction the slots are distinct; for staying particles the slot means nothing.
All inputs are finite; a program needn't handle non-finite values.
Results may differ from a plain program's by a relative error of at most 0.0085.
Values may be sent and summed in bfloat16 or wider, within the bound.
A program may use at most 64 MiB of HBM per device.

v0:
```python
import functools

import jax
import jax.numpy as jnp
from jax import lax
from jax.experimental import pallas as pl
from jax.experimental.pallas import tpu as pltpu
from jax.sharding import PartitionSpec as P

MIG = 4
SLOT_ROWS = 8

norm_eps = 1e-05
F32 = jnp.float32
BF16 = jnp.bfloat16
HIGHEST = lax.Precision.HIGHEST
MESH = pl.DeviceIdType.MESH
AXES = ("gx", "gy", "gz")


def dot(a, b, precision=None):
    return jnp.dot(a, b, preferred_element_type=F32, precision=precision)


def dot_nt(a, b, precision=None):
    return lax.dot_general(
        a, b, (((1,), (1,)), ((), ())), preferred_element_type=F32, precision=precision
    )


def turned(weight):
    return weight.astype(F32).T.astype(weight.dtype)


def normed(values):
    center = values - jnp.mean(values, axis=0, keepdims=True)
    spread = jnp.mean(center * center, axis=0, keepdims=True)
    return center, lax.rsqrt(spread + norm_eps)


def as_column(row, lanes):
    width = row.shape[1]
    square = jnp.broadcast_to(row, (width, width)).T
    return jnp.broadcast_to(square[:, 0:1], (width, lanes))


def fill_outbox(send_hot, latent, outbox_ref):
    outbox_ref[...] = dot_nt(send_hot, latent).astype(BF16).reshape(outbox_ref.shape)


def encode_nodes(kin_ref, send_ref, node_w1, node_w2, latent_ref, hot_ref, square, wide):
    particles = kin_ref.shape[1]
    directions, ghost_count = send_ref.shape
    features = node_w1.shape[0]
    square[...] = jnp.zeros_like(square)
    wide[...] = jnp.zeros_like(wide)
    square[0:features, :] = node_w1[...]
    wide[0:features, :] = kin_ref[3:, :]
    hidden = jnp.maximum(dot(square[...].T, wide[...], HIGHEST), 0.0).astype(BF16)
    center, scale = normed(dot(turned(node_w2[...]), hidden))
    latent_ref[...] = (center * scale).astype(BF16)

    rows = lax.broadcasted_iota(jnp.int32, (ghost_count, ghost_count), 0)
    lanes = lax.broadcasted_iota(jnp.int32, (ghost_count, ghost_count), 1)
    unit = (rows == lanes).astype(F32)
    wanted = dot_nt(unit, send_ref[...].astype(F32), HIGHEST)
    position = lax.broadcasted_iota(jnp.int32, (ghost_count, particles), 1).astype(F32)
    for q in range(directions):
        near = jnp.abs(wanted[:, q : q + 1] - position) < 0.5
        hot_ref[q * ghost_count : (q + 1) * ghost_count, :] = jnp.where(near, 1.0, 0.0).astype(BF16)


def encode_edges(off_ref, index_ref, edge_w1, edge_w2, edge_ref, pair_hot, square, columns):
    width = edge_w2.shape[1]
    particles = off_ref.shape[2]
    pair_slots, rows = pair_hot.shape[:2]
    square[0:4, :] = edge_w1[...]
    first = square[...].T
    for c in range(4):
        columns[c] = jnp.broadcast_to(first[:, c : c + 1], (width, particles))
    second = turned(edge_w2[...])
    row_id = lax.broadcasted_iota(jnp.int32, (rows, particles), 0)

    def one_slot(k, carry):
        x = off_ref[0, pl.ds(k, 1), :]
        y = off_ref[1, pl.ds(k, 1), :]
        z = off_ref[2, pl.ds(k, 1), :]
        pre = columns[0] * x + columns[1] * y + columns[2] * z
        pre = pre + columns[3] * (x * x + y * y + z * z)
        mid = jnp.maximum(pre, 0.0).astype(BF16)
        center, scale = normed(dot(second, mid))
        edge_ref[k] = (center * scale).astype(BF16)
        pair_hot[k] = jnp.where(row_id == index_ref[pl.ds(k, 1), :], 1.0, 0.0).astype(BF16)
        return carry

    lax.fori_loop(0, pair_slots, one_slot, 0, unroll=4)


def prepare(latent_ref, edge_w1, edge_w2, extended, joined):
    width, particles = latent_ref.shape
    latent = latent_ref[...]
    extended[:, :particles] = latent
    joined[:, :width] = turned(edge_w1[:width, :])
    joined[:, width:] = turned(edge_w1[2 * width :, :])
    received = dot(turned(edge_w1[width : 2 * width, :]), latent)
    return latent, received, turned(edge_w2[...])


def update_latent(
    ready, ghost_ref, edge_ref, pair_hot, count_ref, node_w1, node_w2, edge_gain, node_gain,
    extended, joined,
):
    latent, received, second = ready
    width, particles = latent.shape
    pair_slots = edge_ref.shape[0]
    ghosts = ghost_ref[...].reshape(-1, width)
    diagonal = lax.broadcasted_iota(jnp.int32, (width, width), 0) == lax.broadcasted_iota(
        jnp.int32, (width, width), 1
    )
    unit = jnp.where(diagonal, 1.0, 0.0).astype(BF16)
    extended[:, particles:] = dot_nt(unit, ghosts).astype(BF16)
    count = count_ref[...]

    def one_slot(k, total):
        sender = dot(extended[...], pair_hot[k]).astype(BF16)
        both = jnp.concatenate([edge_ref[k], sender], axis=0)
        hidden = jnp.maximum(dot(joined[...], both) + received, 0.0).astype(BF16)
        center, scale = normed(dot(second, hidden))
        return total + center * jnp.where(k < count, scale, 0.0)

    total = lax.fori_loop(
        0, pair_slots, one_slot, jnp.zeros((width, particles), F32), unroll=4
    )
    aggregate = (total * as_column(edge_gain[...], particles)).astype(BF16)
    pre = dot(turned(node_w1[:width, :]), latent) + dot(turned(node_w1[width:, :]), aggregate)
    center, scale = normed(dot(turned(node_w2[...]), jnp.maximum(pre, 0.0).astype(BF16)))
    update = center * scale * as_column(node_gain[...], particles)
    return (latent.astype(F32) + update).astype(BF16)


def finish(
    latent, kin_ref, dir_ref, slot_ref, dec_w1, dec_w2, stayed_ref, leaving_ref, state, reading
):
    state_rows, particles = kin_ref.shape
    hidden = jnp.maximum(dot(turned(dec_w1[...]), latent), 0.0).astype(BF16)
    reading[...] = jnp.zeros_like(reading)
    reading[0:3, :] = dec_w2[...]
    acceleration = dot(reading[...], hidden.astype(F32), HIGHEST)[0:3, :]
    velocity = kin_ref[state_rows - 3 :, :] + acceleration
    state[...] = jnp.zeros_like(state)
    state[0:3, :] = kin_ref[0:3, :] + velocity
    state[3 : state_rows - 3, :] = kin_ref[6:, :]
    state[state_rows - 3 : state_rows, :] = velocity
    staying = dir_ref[...] == 13
    stayed_ref[...] = jnp.where(staying, state[0:state_rows, :], 0.0)
    target = jnp.where(staying, -1, dir_ref[...] * SLOT_ROWS + slot_ref[...])
    row_id = lax.broadcasted_iota(jnp.int32, (27 * SLOT_ROWS, particles), 0)
    picker = jnp.where(row_id == target, 1.0, 0.0)
    leaving_ref[...] = dot_nt(picker, state[...], HIGHEST).reshape(leaving_ref.shape)


def neighbours():
    sizes = [lax.axis_size(axis) for axis in AXES]
    here = [lax.axis_index(axis) for axis in AXES]
    for q in range(27):
        if q == 13:
            continue
        there = [i + s for i, s in zip(here, (q // 9 - 1, q // 3 % 3 - 1, q % 3 - 1))]
        inside = functools.reduce(
            jnp.logical_and, [jnp.logical_and(t >= 0, t < n) for t, n in zip(there, sizes)]
        )
        yield q, tuple(there), inside


def enter(around):
    barrier = pltpu.get_barrier_semaphore()
    for q, there, inside in around:

        @pl.when(inside)
        def _():
            pl.semaphore_signal(barrier, inc=1, device_id=there, device_id_type=MESH)

    peers = 1
    for axis in AXES:
        i, n = lax.axis_index(axis), lax.axis_size(axis)
        peers = peers * (1 + jnp.where(i > 0, 1, 0) + jnp.where(i < n - 1, 1, 0))
    return barrier, peers - 1


def send(around, outbox_ref, inbox_ref, send_sems, recv_sems):
    for q, there, inside in around:

        @pl.when(inside)
        def _():
            pltpu.make_async_remote_copy(
                src_ref=outbox_ref.at[q],
                dst_ref=inbox_ref.at[26 - q],
                send_sem=send_sems.at[q],
                recv_sem=recv_sems.at[26 - q],
                device_id=there,
                device_id_type=MESH,
            ).start()


def land(around, outbox_ref, inbox_ref, send_sems, recv_sems):
    for q, there, inside in around:

        @pl.when(inside)
        def _():
            copy = pltpu.make_async_remote_copy(
                src_ref=outbox_ref.at[q],
                dst_ref=inbox_ref.at[q],
                send_sem=send_sems.at[q],
                recv_sem=recv_sems.at[q],
                device_id=there,
                device_id_type=MESH,
            )
            copy.wait_recv()
            copy.wait_send()


def step_kernel(
    kin_ref, off_ref, index_ref, count_ref, send_ref, dir_ref, slot_ref, enc_node_w1, enc_node_w2,
    enc_edge_w1, enc_edge_w2, edge_w1, edge_w2, node_w1, node_w2, edge_gain, node_gain, dec_w1,
    dec_w2, stayed_ref, arrived_ref, latent_ref, edge_ref, send_hot, pair_hot, outbox, inbox,
    leaving, landed, send_sems, recv_sems, square, wide, columns, extended, joined, reading,
):
    around = list(neighbours())
    for r in range(inbox.shape[0]):
        inbox[r] = jnp.zeros(inbox.shape[1:], inbox.dtype)
    landed[...] = jnp.zeros_like(landed)
    barrier, peers = enter(around)
    encode_nodes(
        kin_ref, send_ref, enc_node_w1, enc_node_w2, latent_ref, send_hot, square, wide
    )
    fill_outbox(send_hot[...], latent_ref[...], outbox.at[0])
    pl.semaphore_wait(barrier, peers)
    rounds = edge_w1.shape[0]
    for r in range(rounds):
        path = (outbox.at[r], inbox.at[r], send_sems.at[r], recv_sems.at[r])
        send(around, *path)
        if r == 0:
            encode_edges(
                off_ref, index_ref, enc_edge_w1, enc_edge_w2, edge_ref, pair_hot, square, columns
            )
        ready = prepare(latent_ref, edge_w1.at[r], edge_w2.at[r], extended, joined)
        land(around, *path)
        latent = update_latent(
            ready, inbox.at[r], edge_ref, pair_hot, count_ref, node_w1.at[r], node_w2.at[r],
            edge_gain.at[r : r + 1], node_gain.at[r : r + 1], extended, joined,
        )
        latent_ref[...] = latent
        if r < rounds - 1:
            fill_outbox(send_hot[...], latent, outbox.at[r + 1])
    finish(
        latent, kin_ref, dir_ref, slot_ref, dec_w1, dec_w2, stayed_ref, leaving, wide, reading
    )
    path = (leaving, landed, send_sems.at[rounds], recv_sems.at[rounds])
    send(around, *path)
    land(around, *path)
    state_rows = kin_ref.shape[0]
    turned_rows = landed[...].reshape(27 * SLOT_ROWS, landed.shape[2])
    spread = lax.broadcasted_iota(jnp.int32, (27 * MIG, 27 * SLOT_ROWS), 0)
    source = lax.broadcasted_iota(jnp.int32, (27 * MIG, 27 * SLOT_ROWS), 1)
    lane = spread // MIG * SLOT_ROWS + spread % MIG
    compact = jnp.where(lane == source, 1.0, 0.0)
    unit_rows = lax.broadcasted_iota(jnp.int32, (landed.shape[2],) * 2, 0)
    unit_lanes = lax.broadcasted_iota(jnp.int32, (landed.shape[2],) * 2, 1)
    unit = jnp.where(unit_rows == unit_lanes, 1.0, 0.0)
    across = dot_nt(unit, turned_rows, HIGHEST)
    arrived_ref[...] = dot_nt(across, compact, HIGHEST)[0:state_rows, :]


def on_device(
    kinematics,
    pair_offsets,
    pair_index,
    neighbour_count,
    send_rows,
    migrate_dir,
    migrate_slot,
    enc_node_w1,
    enc_node_w2,
    enc_edge_w1,
    enc_edge_w2,
    edge_w1,
    edge_w2,
    node_w1,
    node_w2,
    edge_gain,
    node_gain,
    dec_w1,
    dec_w2,
):
    width = enc_node_w2.shape[1]
    pair_slots, particles = pair_index.shape
    ghost_count = send_rows.shape[1]
    state_rows = kinematics.shape[0]
    rounds = edge_w1.shape[0]
    ghost_rows = 27 * ghost_count
    total_rows = particles + ghost_rows
    operands = (
        kinematics, pair_offsets, pair_index, neighbour_count.reshape(1, particles), send_rows,
        migrate_dir.reshape(1, particles), migrate_slot.reshape(1, particles), enc_node_w1,
        enc_node_w2, enc_edge_w1, enc_edge_w2, edge_w1, edge_w2, node_w1, node_w2, edge_gain,
        node_gain, dec_w1, dec_w2,
    )
    vmem = pl.BlockSpec(memory_space=pltpu.VMEM)
    return tuple(
        pl.pallas_call(
            step_kernel,
            name="step",
            in_specs=[vmem] * len(operands),
            out_specs=[vmem, vmem],
            out_shape=[
                jax.ShapeDtypeStruct((state_rows, particles), F32),
                jax.ShapeDtypeStruct((state_rows, 27 * MIG), F32),
            ],
            scratch_shapes=[
                pltpu.VMEM((width, particles), BF16),
                pltpu.VMEM((pair_slots, width, particles), BF16),
                pltpu.VMEM((ghost_rows, particles), BF16),
                pltpu.VMEM((pair_slots, total_rows, particles), BF16),
                pltpu.VMEM((rounds, 27, ghost_count, width), BF16),
                pltpu.VMEM((rounds, 27, ghost_count, width), BF16),
                pltpu.VMEM((27, SLOT_ROWS, width), F32),
                pltpu.VMEM((27, SLOT_ROWS, width), F32),
                pltpu.SemaphoreType.DMA((rounds + 1, 27)),
                pltpu.SemaphoreType.DMA((rounds + 1, 27)),
                pltpu.VMEM((width, width), F32),
                pltpu.VMEM((width, particles), F32),
                pltpu.VMEM((4, width, particles), F32),
                pltpu.VMEM((width, total_rows), BF16),
                pltpu.VMEM((width, 2 * width), BF16),
                pltpu.VMEM((8, width), F32),
            ],
            compiler_params=pltpu.CompilerParams(collective_id=0, has_side_effects=True),
        )(*operands)
    )


def solution(mesh):
    split = ("gx", "gy", "gz")
    return jax.shard_map(
        on_device,
        mesh=mesh,
        in_specs=(
            P(None, split),
            P(None, None, split),
            P(None, split),
            P(split),
            P(None, split),
            P(split),
            P(split),
        )
        + (P(),) * 12,
        out_specs=(P(None, split), P(None, split)),
        check_vma=False,
    )
```

profile of v0, /device:TPU:1, one launch (start us, length us, event | category | flops | bytes accessed | tf_op | source)
XLA Modules:
  0.0 53.6 jit_solution(10741407108336824909)
XLA Ops:
  0.6 1.4 %copy.21.send_ref = s32[27,16]{1,0:T(8,128)} copy(s32[27,16]{0,1:T(8,128)} %param.23) | data formatting | bytes 3456 | tf_op args[4]
  2.0 49.6 %step.1 = (f32[18,256]{1,0:T(8,128)}, f32[18,108]{1,0:T(8,128)}) custom-call(f32[18,256]{1,0:T(8,128)} %kin_ref.1, f32[3,16,256]{2,1,0:T(8,128)} %off_ref.1, s32[16,256]{1,0:T(8,128)} %index_ref.1, s32[1,256]{1,0:T(1,128)} %bitcast.3, s32[27,16]{1,0:T(8,128)} %copy.21.send_ref, s32[1,256]{1,0:T(1,128)} %bitcast.4, s32[1,256]{1,0:T(1,128)} %bitcast.5, ...), custom_call_target="tpu_custom_call" | custom-call | tf_op jit(solution)/shard_map/step/pallas_call | solution.py:310
  51.7 0.0 copy-start
  51.7 1.4 %copy.24 = f32[18,256]{1,0:T(8,128)} copy(f32[18,256]{1,0:T(8,128)} %get-tuple-element.4) | data formatting | bytes 36864
  53.0 0.0 copy-done
  53.0 0.6 %copy.25 = f32[18,108]{1,0:T(8,128)} copy(f32[18,108]{1,0:T(8,128)S(1)} %copy-done) | data formatting | bytes 15552
Async XLA Ops:
  51.7 1.4 %copy-start = (f32[18,108]{1,0:T(8,128)S(1)}, f32[18,108]{1,0:T(8,128)}, u32[]{:S(2)}) copy-start(f32[18,108]{1,0:T(8,128)} %get-tuple-element.5) | copy-start | bytes 23332
where the time goes:
time: 53.9 us; the launch traced here: 53.6 us
  Pallas kernels  49.6 us (92%)
  local copies, waits for them, and re-layouts  3.34 us (6%)
  between operations  0.65 us (1%)
    pallas_call x1, Pallas kernels, on_device(): pl.pallas_call(step_kernel, name='step', in_specs=[vmem] * len(operands),...  49.6 us
    unnamed x5, local copies, waits for them, and re-layouts  3.34 us

commit v1 on v0

v1 whole, which is shorter than its diff:
```python
import functools

import jax
import jax.numpy as jnp
from jax import lax
from jax.experimental import pallas as pl
from jax.experimental.pallas import tpu as pltpu
from jax.sharding import PartitionSpec as P

MIG = 4

norm_eps = 1e-05
F32 = jnp.float32
BF16 = jnp.bfloat16
I32 = jnp.int32
MESH = pl.DeviceIdType.MESH
AXES = ("gx", "gy", "gz")


def dot(a, b):
    return jnp.dot(a, b, preferred_element_type=F32)


def dot_nt(a, b):
    return lax.dot_general(a, b, (((1,), (1,)), ((), ())), preferred_element_type=F32)


def iota(shape, axis):
    return lax.broadcasted_iota(I32, shape, axis)


def head(values):
    return values.astype(BF16).astype(F32)


def inverse_spread(square_sum, width):
    return lax.rsqrt(square_sum * (1.0 / width) + norm_eps)


def fold_rows(values):
    rows, lanes = values.shape
    return jnp.sum(values.reshape(rows // 8, 8, lanes), axis=0)


def normed(center):
    return center * inverse_spread(jnp.sum(center * center, axis=0, keepdims=True), center.shape[0])


class Slots:
    def __init__(self, sizes):
        self.folded = sizes[0] == 2
        steps = [(q // 9 - 1, q // 3 % 3 - 1, q % 3 - 1) for q in range(27) if q != 13]
        if self.folded:
            steps = [s for s in steps if s[0] >= 0]
        first = (1, 0, 0)
        self.steps = [first] + sorted((s for s in steps if s != first), key=lambda s: -sum(map(abs, s)))
        self.number = {s: n for n, s in enumerate(self.steps)}

    def __len__(self):
        return len(self.steps)

    def opposite(self, n):
        x, y, z = self.steps[n]
        return self.number[(x if self.folded else -x, -y, -z)]

    def direction(self, n):
        x, y, z = self.steps[n]
        rest = (y + 1) * 3 + z + 1
        if self.folded and x == 1:
            return rest + 18 - 18 * lax.axis_index("gx")
        return rest + (x + 1) * 9

    def place(self, n):
        x, y, z = self.steps[n]
        return (x if self.folded else x + 1) * 9 + (y + 1) * 3 + z + 1

    def peer(self, n):
        x, y, z = self.steps[n]
        i, j, k = (lax.axis_index(axis) for axis in AXES)
        there = (1 - i if x else i) if self.folded else i + x, j + y, k + z
        tests = []
        for axis, step, position in zip(AXES, self.steps[n], there):
            if step and not (self.folded and axis == "gx"):
                tests.append(jnp.logical_and(position >= 0, position < lax.axis_size(axis)))
        return there, functools.reduce(jnp.logical_and, tests) if tests else None


def guarded(inside, action):
    if inside is None:
        action()
    else:
        pl.when(inside)(action)


def enter(slots):
    barrier = pltpu.get_barrier_semaphore()
    for n in range(len(slots)):
        there, inside = slots.peer(n)
        guarded(inside, lambda: pl.semaphore_signal(barrier, inc=1, device_id=there, device_id_type=MESH))
    peers = 1
    for axis in AXES:
        i, n = lax.axis_index(axis), lax.axis_size(axis)
        peers = peers * (1 + jnp.where(i > 0, 1, 0) + jnp.where(i < n - 1, 1, 0))
    return barrier, peers - 1


def remote(source, target, send_sem, recv_sem, there):
    return pltpu.make_async_remote_copy(
        src_ref=source, dst_ref=target, send_sem=send_sem, recv_sem=recv_sem,
        device_id=there, device_id_type=MESH,
    )


def send(slots, outbox, inbox, send_sems, recv_sems, by_direction=False):
    for n in list(range(1, len(slots))) + [0]:
        there, inside = slots.peer(n)
        far = slots.opposite(n)
        q = slots.direction(n) if by_direction else n
        into = 26 - q if by_direction else far
        copy = remote(outbox.at[q], inbox.at[into], send_sems.at[n], recv_sems.at[far], there)
        guarded(inside, copy.start)


def land(slots, numbers, outbox, inbox, send_sems, recv_sems, by_direction=False):
    for n in numbers:
        there, inside = slots.peer(n)
        q = slots.direction(n) if by_direction else n
        copy = remote(outbox.at[q], inbox.at[q], send_sems.at[n], recv_sems.at[n], there)

        def both():
            copy.wait_recv()
            copy.wait_send()

        guarded(inside, both)


def encode_nodes(kin_ref, node_w1, node_w2, center_of, square, wide):
    features = node_w1.shape[0]
    square[...] = jnp.zeros_like(square)
    wide[...] = jnp.zeros_like(wide)
    first = node_w1[...]
    square[0:features, :] = first
    square[16 : 16 + features, :] = first
    square[32 : 32 + features, :] = first - head(first)
    moves = kin_ref[3:, :]
    wide[0:features, :] = moves
    wide[16 : 16 + features, :] = moves - head(moves)
    wide[32 : 32 + features, :] = moves
    hidden = jnp.maximum(dot(square[...].T.astype(BF16), wide[...].astype(BF16)), 0.0).astype(BF16)
    second = dot_nt(center_of, node_w2[...]).astype(BF16)
    return normed(dot(second, hidden)).astype(BF16)


def fill_send_hot(slots, send_ref, send_hot):
    ghosts = send_ref.shape[0]
    particles = send_hot.shape[1]
    position = iota((ghosts, particles), 1)
    for n in range(len(slots)):
        x, y, z = slots.steps[n]
        q = slots.place(n) + (9 if slots.folded else 0)
        wanted = send_ref[:, q : q + 1]
        if slots.folded and x == 1:
            wanted = jnp.where(lax.axis_index("gx") == 0, wanted, send_ref[:, q - 18 : q - 17])
        send_hot[n * ghosts : (n + 1) * ghosts, :] = jnp.where(position == wanted, 1.0, 0.0).astype(BF16)


def prepare_indices(slots, index_ref, local_code, ghost_code, row_code, ghosts):
    pair_slots, particles = index_ref.shape
    lanes = row_code.shape[1]
    index = index_ref[...]
    ghost = index - particles
    half = 9 * ghosts
    if slots.folded:
        code = jnp.where(ghost < half, ghost + half, ghost - half) - half
    else:
        code = ghost - 3 * half // 2
    local_code[...] = index.astype(F32)
    ghost_code[...] = jnp.where(index < particles, 255, code).astype(F32)
    steps = iota((16, lanes), 0)
    for b in range(particles // 16):
        row_code[16 * b : 16 * (b + 1), :] = (steps + 16 * b).astype(F32).astype(BF16)
    shift = half if slots.folded else 3 * half // 2
    rows = iota((ghosts, lanes), 0)
    for n in range(len(slots)):
        start = particles + n * ghosts
        row_code[start : start + ghosts, :] = (rows + (slots.place(n) * ghosts - shift)).astype(F32).astype(BF16)


def fill_pair_hot(k, local_code, ghost_code, row_code, near, far, width, ghosts):
    particles = near.shape[2]
    one = jnp.ones((16, particles), BF16)
    zero = jnp.zeros((16, particles), BF16)
    local = jnp.broadcast_to(local_code[pl.ds(k, 1), :], (16, particles)).astype(BF16)
    ghost = jnp.broadcast_to(ghost_code[pl.ds(k, 1), :], (16, particles)).astype(BF16)

    def block(row, code):
        return jnp.where(row_code[row : row + 16, :] == code, one, zero)

    for b in range(particles // 16):
        near[k, 16 * b : 16 * (b + 1), :] = block(16 * b, local)
    for b in range(ghosts // 16):
        start = particles + width + 16 * b
        near[k, start : start + 16, :] = block(particles + 16 * b, ghost)
    for b in range(far.shape[1] // 16):
        far[k, 16 * b : 16 * (b + 1), :] = block(particles + ghosts + 16 * b, ghost)


def edge_features(off_ref, edge_w1, square, feature):
    pair_slots = off_ref.shape[1]
    width = edge_w1.shape[1]
    x, y, z = off_ref[0], off_ref[1], off_ref[2]
    terms = (x, y, z, x * x + y * y + z * z)
    rows = 4 * pair_slots
    for c, term in enumerate(terms):
        high = term.astype(BF16)
        low = (term - high.astype(F32)).astype(BF16)
        feature[c * pair_slots : (c + 1) * pair_slots, :] = high
        feature[rows + c * pair_slots : rows + (c + 1) * pair_slots, :] = low
        feature[2 * rows + c * pair_slots : 2 * rows + (c + 1) * pair_slots, :] = high
    first = edge_w1[...]
    square[0:4, :] = first
    square[4:8, :] = first
    square[8:12, :] = first - head(first)
    spread_row = iota((width, 3 * rows), 0)
    spread_lane = iota((width, 3 * rows), 1)
    spread = jnp.where(spread_lane // pair_slots == spread_row, 1.0, 0.0).astype(BF16)
    return dot(square[...].T.astype(BF16), spread)


def step_kernel(
    kin_ref, off_ref, index_ref, count_ref, send_ref, dir_ref, slot_ref, enc_node_w1, enc_node_w2,
    enc_edge_w1, enc_edge_w2, edge_w1, edge_w2, node_w1, node_w2, edge_gain, node_gain, dec_w1,
    dec_w2, stayed_ref, arrived_ref, outbox, inbox, leaving, landed, send_sems, recv_sems,
    square, wide, feature, base, local_code, ghost_code, row_code, send_hot, near, far,
    hidden, partial, squares, near_left, far_left, received, first_t, second_c, node_t, node_c,
    gains, both, state, rows,
):
    sizes = [lax.axis_size(axis) for axis in AXES]
    slots = Slots(sizes)
    width = enc_node_w2.shape[1]
    state_rows, particles = kin_ref.shape
    pair_slots = index_ref.shape[0]
    ghosts = send_ref.shape[0]
    rounds = edge_w1.shape[0]

    for r in range(rounds):
        inbox[r] = jnp.zeros(inbox.shape[1:], inbox.dtype)
    landed[...] = jnp.zeros_like(landed)
    barrier, peers = enter(slots)

    diagonal = iota((width, width), 0) == iota((width, width), 1)
    unit = jnp.where(diagonal, 1.0, 0.0).astype(BF16)
    center_of = jnp.where(diagonal, 1.0 - 1.0 / width, -1.0 / width).astype(BF16)

    fill_send_hot(slots, send_ref, send_hot)
    latent = encode_nodes(kin_ref, enc_node_w1, enc_node_w2, center_of, square, wide)
    both[0:width, :] = latent
    outbox[0] = dot_nt(send_hot[...], latent).astype(BF16).reshape(outbox.shape[1:])
    pl.semaphore_wait(barrier, peers)

    def path(r):
        return outbox.at[r], inbox.at[r], send_sems.at[r], recv_sems.at[r]

    def turn_weights(r):
        first_t[r] = dot_nt(unit, edge_w1[r]).astype(BF16)
        second_c[r] = dot_nt(center_of, edge_w2[r]).astype(BF16)
        node_t[r] = dot_nt(unit, node_w1[r]).astype(BF16)
        node_c[r] = dot_nt(center_of, node_w2[r]).astype(BF16)

    def local_part(r):
        weights = first_t.at[r]
        now = both[0:width, :]
        received[...] = dot(weights[:, width : 2 * width], now)
        near_left[:, 0:particles] = dot(weights[:, 2 * width :], now).astype(BF16)
        near_left[:, particles : particles + width] = weights[:, 0:width]

    for r in range(rounds):
        send(slots, *path(r))
        if r == 0:
            base[...] = edge_features(off_ref, enc_edge_w1, square, feature).astype(BF16)
            enc_second = dot_nt(center_of, enc_edge_w2[...]).astype(BF16)
            prepare_indices(slots, index_ref, local_code, ghost_code, row_code, ghosts)
            slot_of = iota(base.shape, 1) % pair_slots

            def first_edge(k, carry):
                left = jnp.where(slot_of == k, base[...].astype(F32), 0.0).astype(BF16)
                hidden[k] = jnp.maximum(dot(left, feature[...]), 0.0).astype(BF16)
                return carry

            lax.fori_loop(0, pair_slots, first_edge, 0, unroll=4)

            def second_edge(k, carry):
                fresh = normed(dot(enc_second, hidden[k])).astype(BF16)
                near[k, particles : particles + width, :] = fresh
                fill_pair_hot(k, local_code, ghost_code, row_code, near, far, width, ghosts)
                return carry

            lax.fori_loop(0, pair_slots, second_edge, 0, unroll=4)
            turn_weights(0)
            square[0:rounds, :] = edge_gain[...]
            square[rounds : 2 * rounds, :] = node_gain[...]
            columns = square[...].T
            for g in range(2 * rounds):
                gains[g] = jnp.broadcast_to(columns[:, g : g + 1], (width, width))
        local_part(r)
        land(slots, [0], *path(r))
        first_ghosts = inbox[r, 0]
        near_left[:, particles + width :] = dot_nt(first_t[r, :, 2 * width :], first_ghosts).astype(BF16)

        def early(k, carry):
            partial[k] = dot(near_left[...], near[k]) + received[...]
            return carry

        lax.fori_loop(0, pair_slots, early, 0, unroll=4)
        if r + 1 < rounds:
            turn_weights(r + 1)
        land(slots, range(1, len(slots)), *path(r))
        late_ghosts = inbox[r, 1:].reshape(-1, width)
        far_left[...] = dot_nt(first_t[r, :, 2 * width :], late_ghosts).astype(BF16)

        def late(k, carry):
            hidden[k] = jnp.maximum(partial[k] + dot(far_left[...], far[k]), 0.0).astype(BF16)
            return carry

        lax.fori_loop(0, pair_slots, late, 0, unroll=4)

        def second(k, carry):
            center = dot(second_c[r], hidden[k])
            partial[k] = center
            scale = inverse_spread(jnp.sum(center * center, axis=0, keepdims=True), width)
            squares[k] = jnp.broadcast_to(jnp.where(k < count_ref[...], scale, 0.0), squares.shape[1:])
            return carry

        lax.fori_loop(0, pair_slots, second, 0, unroll=4)

        edge_column = jnp.concatenate([gains[r]] * (particles // width), axis=1)
        node_column = jnp.concatenate([gains[rounds + r]] * (particles // width), axis=1)
        for f in range(0, width, 8):
            total = partial[0, f : f + 8, :] * squares[0]
            for k in range(1, pair_slots):
                total = total + partial[k, f : f + 8, :] * squares[k]
            received[f : f + 8, :] = total
        both[width : 2 * width, :] = (received[...] * edge_column).astype(BF16)
        middle = jnp.maximum(dot(node_t[r], both[...]), 0.0).astype(BF16)
        update = normed(dot(node_c[r], middle)) * node_column
        latent = (both[0:width, :].astype(F32) + update).astype(BF16)
        both[0:width, :] = latent
        if r + 1 < rounds:
            outbox[r + 1] = dot_nt(send_hot[...], latent).astype(BF16).reshape(outbox.shape[1:])

    reading = dec_w2[...]
    wide[...] = jnp.zeros_like(wide)
    wide[0:3, 0:width] = reading
    wide[8:11, 0:width] = reading - head(reading)
    wide[16:19, 0:width] = reading - head(reading) - head(reading - head(reading))
    readout = wide[0:32, 0:width].astype(BF16)
    decoded = jnp.maximum(dot(dot_nt(unit, dec_w1[...]).astype(BF16), latent), 0.0).astype(BF16)
    parts = dot(readout, decoded)
    velocity = kin_ref[state_rows - 3 :, :] + (parts[0:3, :] + (parts[8:11, :] + parts[16:19, :]))
    state[...] = jnp.zeros_like(state)
    state[0:3, :] = kin_ref[0:3, :] + velocity
    state[3 : state_rows - 3, :] = kin_ref[6:, :]
    state[state_rows - 3 : state_rows, :] = velocity
    staying = dir_ref[...] == 13
    target = jnp.where(staying, -1, dir_ref[...] * MIG + slot_ref[...])
    picker = jnp.where(iota((rows.shape[0], particles), 0) == target, 1.0, 0.0).astype(BF16)
    whole = state[...]
    high = whole.astype(BF16)
    rest = whole - high.astype(F32)
    middle = rest.astype(BF16)
    low = (rest - middle.astype(F32)).astype(BF16)
    rows[:, 0 : state.shape[0]] = dot_nt(picker, high) + dot_nt(picker, middle) + dot_nt(picker, low)
    for q in range(27):
        leaving[q] = rows[MIG * q : MIG * (q + 1), :]
    migration = (leaving, landed, send_sems.at[rounds], recv_sems.at[rounds])
    send(slots, *migration, by_direction=True)
    stayed_ref[...] = jnp.where(staying, state[0:state_rows, :], 0.0)
    land(slots, range(len(slots)), *migration, by_direction=True)
    for q in range(27):
        rows[MIG * q : MIG * (q + 1), :] = landed[q]
    arrived_ref[...] = rows[...].T[0:state_rows, 0 : 27 * MIG]


def on_device(
    kinematics, pair_offsets, pair_index, neighbour_count, send_rows, migrate_dir, migrate_slot,
    enc_node_w1, enc_node_w2, enc_edge_w1, enc_edge_w2, edge_w1, edge_w2, node_w1, node_w2,
    edge_gain, node_gain, dec_w1, dec_w2,
):
    width = enc_node_w2.shape[1]
    pair_slots, particles = pair_index.shape
    ghosts = send_rows.shape[1]
    state_rows = kinematics.shape[0]
    rounds = edge_w1.shape[0]
    slot_count = len(Slots([lax.axis_size(axis) for axis in AXES]))
    near_rows = particles + width + ghosts
    far_rows = (slot_count - 1) * ghosts
    operands = (
        kinematics, pair_offsets, pair_index, neighbour_count.reshape(1, particles), send_rows.T,
        migrate_dir.reshape(1, particles), migrate_slot.reshape(1, particles), enc_node_w1,
        enc_node_w2, enc_edge_w1, enc_edge_w2, edge_w1, edge_w2, node_w1, node_w2, edge_gain,
        node_gain, dec_w1, dec_w2,
    )
    vmem = pl.BlockSpec(memory_space=pltpu.VMEM)
    return tuple(
        pl.pallas_call(
            step_kernel,
            name="step",
            in_specs=[vmem] * len(operands),
            out_specs=[vmem, vmem],
            out_shape=[
                jax.ShapeDtypeStruct((state_rows, particles), F32),
                jax.ShapeDtypeStruct((state_rows, 27 * MIG), F32),
            ],
            scratch_shapes=[
                pltpu.VMEM((rounds, slot_count, ghosts, width), BF16),
                pltpu.VMEM((rounds, slot_count, ghosts, width), BF16),
                pltpu.VMEM((27, MIG, width), F32),
                pltpu.VMEM((27, MIG, width), F32),
                pltpu.SemaphoreType.DMA((rounds + 1, slot_count)),
                pltpu.SemaphoreType.DMA((rounds + 1, slot_count)),
                pltpu.VMEM((width, width), F32),
                pltpu.VMEM((width, particles), F32),
                pltpu.VMEM((12 * pair_slots, particles), BF16),
                pltpu.VMEM((width, 12 * pair_slots), BF16),
                pltpu.VMEM((pair_slots, particles), F32),
                pltpu.VMEM((pair_slots, particles), F32),
                pltpu.VMEM((particles + slot_count * ghosts, particles), BF16),
                pltpu.VMEM((slot_count * ghosts, particles), BF16),
                pltpu.VMEM((pair_slots, near_rows, particles), BF16),
                pltpu.VMEM((pair_slots, far_rows, particles), BF16),
                pltpu.VMEM((pair_slots, width, particles), BF16),
                pltpu.VMEM((pair_slots, width, particles), F32),
                pltpu.VMEM((pair_slots, 8, particles), F32),
                pltpu.VMEM((width, near_rows), BF16),
                pltpu.VMEM((width, far_rows), BF16),
                pltpu.VMEM((width, particles), F32),
                pltpu.VMEM((rounds, width, 3 * width), BF16),
                pltpu.VMEM((rounds, width, width), BF16),
                pltpu.VMEM((rounds, width, 2 * width), BF16),
                pltpu.VMEM((rounds, width, width), BF16),
                pltpu.VMEM((2 * rounds, width, width), F32),
                pltpu.VMEM((2 * width, particles), BF16),
                pltpu.VMEM((32, particles), F32),
                pltpu.VMEM((width, width), F32),
            ],
            compiler_params=pltpu.CompilerParams(collective_id=0, has_side_effects=True),
        )(*operands)
    )


def solution(mesh):
    split = ("gx", "gy", "gz")
    return jax.shard_map(
        on_device,
        mesh=mesh,
        in_specs=(
            P(None, split),
            P(None, None, split),
            P(None, split),
            P(split),
            P(None, split),
            P(split),
            P(split),
        )
        + (P(),) * 12,
        out_specs=(P(None, split), P(None, split)),
        check_vma=False,
    )
```

time: 53.9 us -> 35.6 us (0.66)
  Pallas kernels: 49.6 us -> 32.8 us
  local copies, waits for them, and re-layouts: 3.34 us -> 1.96 us
    pallas_call x1, Pallas kernels: 49.6 us -> 32.8 us  [on_device(): pl.pallas_call(step_kernel, name='step', in_specs=[vmem] * len(operands),...]
    unnamed x5 -> x4, local copies, waits for them, and re-layouts: 3.34 us -> 1.96 us
where the time goes in v1:
time: 35.6 us; the launch traced here: 35.4 us
  Pallas kernels  32.8 us (92%)
  local copies, waits for them, and re-layouts  1.96 us (6%)
  between operations  0.66 us (2%)
    pallas_call x1, Pallas kernels, on_device(): pl.pallas_call(step_kernel, name='step', in_specs=[vmem] * len(operands),...  32.8 us
    unnamed x4, local copies, waits for them, and re-layouts  1.96 us

profile of v1, /device:TPU:1, one launch (start us, length us, event | category | flops | bytes accessed | tf_op | source)
XLA Modules:
  0.0 35.4 jit_solution(2795050606510242521)
XLA Ops:
  0.6 32.8 %step.1 = (f32[18,256]{1,0:T(8,128)}, f32[18,108]{1,0:T(8,128)}) custom-call(f32[18,256]{1,0:T(8,128)} %kin_ref.1, f32[3,16,256]{2,1,0:T(8,128)} %off_ref.1, s32[16,256]{1,0:T(8,128)} %index_ref.1, s32[1,256]{1,0:T(1,128)} %bitcast.5, s32[16,27]{1,0:T(8,128)} %bitcast.4, s32[1,256]{1,0:T(1,128)} %bitcast.6, s32[1,256]{1,0:T(1,128)} %bitcast.7, ...), custom_call_target="tpu_custom_call" | custom-call | tf_op jit(solution)/shard_map/step/pallas_call | solution.py:405
  33.4 0.0 copy-start
  33.4 1.4 %copy.23 = f32[18,256]{1,0:T(8,128)} copy(f32[18,256]{1,0:T(8,128)} %get-tuple-element.4) | data formatting | bytes 36864
  34.8 0.0 copy-done
  34.8 0.6 %copy.24 = f32[18,108]{1,0:T(8,128)} copy(f32[18,108]{1,0:T(8,128)S(1)} %copy-done) | data formatting | bytes 15552
Async XLA Ops:
  33.4 1.4 %copy-start = (f32[18,108]{1,0:T(8,128)S(1)}, f32[18,108]{1,0:T(8,128)}, u32[]{:S(2)}) copy-start(f32[18,108]{1,0:T(8,128)} %get-tuple-element.5) | copy-start | bytes 23332

commit v2 on v1

--- a/solution.py
+++ b/solution.py
@@ -52,8 +52,9 @@
         steps = [(q // 9 - 1, q // 3 % 3 - 1, q % 3 - 1) for q in range(27) if q != 13]
         if self.folded:
             steps = [s for s in steps if s[0] >= 0]
-        first = (1, 0, 0)
-        self.steps = [first] + sorted((s for s in steps if s != first), key=lambda s: -sum(map(abs, s)))
+        hops = lambda step: sum(map(abs, step))
+        self.steps = sorted(steps, key=hops)
+        self.faces = sum(hops(step) == 1 for step in steps)
         self.number = {s: n for n, s in enumerate(self.steps)}
 
     def __len__(self):
@@ -90,6 +91,28 @@
         action()
     else:
         pl.when(inside)(action)
+
+
+def clear(slots, inbox, landed):
+    for n in range(len(slots)):
+        inside = slots.peer(n)[1]
+        if inside is not None:
+
+            @pl.when(jnp.logical_not(inside))
+            def _():
+                for r in range(inbox.shape[0]):
+                    inbox[r, n] = jnp.zeros(inbox.shape[2:], inbox.dtype)
+
+    position = [lax.axis_index(axis) for axis in AXES]
+    for q in range(27):
+        tests = [jnp.full((), q == 13)]
+        for i, axis, step in zip(position, AXES, (q // 9 - 1, q // 3 % 3 - 1, q % 3 - 1)):
+            if step:
+                tests.append(i == (0 if step < 0 else lax.axis_size(axis) - 1))
+
+        @pl.when(functools.reduce(jnp.logical_or, tests))
+        def _():
+            landed[q] = jnp.zeros(landed.shape[1:], landed.dtype)
 
 
 def enter(slots):
@@ -112,7 +135,7 @@
 
 
 def send(slots, outbox, inbox, send_sems, recv_sems, by_direction=False):
-    for n in list(range(1, len(slots))) + [0]:
+    for n in reversed(range(len(slots))):
         there, inside = slots.peer(n)
         far = slots.opposite(n)
         q = slots.direction(n) if by_direction else n
@@ -186,8 +209,9 @@
         row_code[start : start + ghosts, :] = (rows + (slots.place(n) * ghosts - shift)).astype(F32).astype(BF16)
 
 
-def fill_pair_hot(k, local_code, ghost_code, row_code, near, far, width, ghosts):
+def fill_pair_hot(k, local_code, ghost_code, row_code, own, near, far, width):
     particles = near.shape[2]
+    near_ghosts = near.shape[1] - width
     one = jnp.ones((16, particles), BF16)
     zero = jnp.zeros((16, particles), BF16)
     local = jnp.broadcast_to(local_code[pl.ds(k, 1), :], (16, particles)).astype(BF16)
@@ -197,12 +221,12 @@
         return jnp.where(row_code[row : row + 16, :] == code, one, zero)
 
     for b in range(particles // 16):
-        near[k, 16 * b : 16 * (b + 1), :] = block(16 * b, local)
-    for b in range(ghosts // 16):
-        start = particles + width + 16 * b
+        own[k, 16 * b : 16 * (b + 1), :] = block(16 * b, local)
+    for b in range(near_ghosts // 16):
+        start = width + 16 * b
         near[k, start : start + 16, :] = block(particles + 16 * b, ghost)
     for b in range(far.shape[1] // 16):
-        far[k, 16 * b : 16 * (b + 1), :] = block(particles + ghosts + 16 * b, ghost)
+        far[k, 16 * b : 16 * (b + 1), :] = block(particles + near_ghosts + 16 * b, ghost)
 
 
 def edge_features(off_ref, edge_w1, square, feature):
@@ -227,31 +251,42 @@
     return dot(square[...].T.astype(BF16), spread)
 
 
-def step_kernel(
-    kin_ref, off_ref, index_ref, count_ref, send_ref, dir_ref, slot_ref, enc_node_w1, enc_node_w2,
-    enc_edge_w1, enc_edge_w2, edge_w1, edge_w2, node_w1, node_w2, edge_gain, node_gain, dec_w1,
-    dec_w2, stayed_ref, arrived_ref, outbox, inbox, leaving, landed, send_sems, recv_sems,
-    square, wide, feature, base, local_code, ghost_code, row_code, send_hot, near, far,
-    hidden, partial, squares, near_left, far_left, received, first_t, second_c, node_t, node_c,
-    gains, both, state, rows,
-):
-    sizes = [lax.axis_size(axis) for axis in AXES]
-    slots = Slots(sizes)
+def step_kernel(slots, *refs):
+    operands, results, scratch = refs[:19], refs[19:21], refs[21:]
+    (
+        kin_ref, off_ref, index_ref, count_ref, send_ref, dir_ref, slot_ref, enc_node_w1, enc_node_w2,
+        enc_edge_w1, enc_edge_w2, edge_w1, edge_w2, node_w1, node_w2, edge_gain, node_gain, dec_w1,
+        dec_w2,
+    ) = copies = scratch[:19]
+    stayed_ref, arrived_ref = results
+    (
+        copy_sems, outbox, inbox, leaving, landed, send_sems, recv_sems, square, wide, feature, base,
+        local_code, ghost_code, row_code, send_hot, own, near, far, hidden, partial, squares, own_left,
+        near_left, far_left, received, first_t, second_c, node_t, node_c, gains, both, state, rows,
+    ) = scratch[19:]
     width = enc_node_w2.shape[1]
     state_rows, particles = kin_ref.shape
     pair_slots = index_ref.shape[0]
     ghosts = send_ref.shape[0]
     rounds = edge_w1.shape[0]
-
-    for r in range(rounds):
-        inbox[r] = jnp.zeros(inbox.shape[1:], inbox.dtype)
-    landed[...] = jnp.zeros_like(landed)
+    faces = slots.faces
+
     barrier, peers = enter(slots)
+    fetches = [
+        pltpu.make_async_copy(source, target, copy_sems.at[n])
+        for n, (source, target) in enumerate(zip(operands, copies))
+    ]
+    urgent = [4, 0, 7, 8]
+    for n in urgent + [n for n in range(19) if n not in urgent]:
+        fetches[n].start()
+    clear(slots, inbox, landed)
 
     diagonal = iota((width, width), 0) == iota((width, width), 1)
     unit = jnp.where(diagonal, 1.0, 0.0).astype(BF16)
     center_of = jnp.where(diagonal, 1.0 - 1.0 / width, -1.0 / width).astype(BF16)
 
+    for n in urgent:
+        fetches[n].wait()
     fill_send_hot(slots, send_ref, send_hot)
     latent = encode_nodes(kin_ref, enc_node_w1, enc_node_w2, center_of, square, wide)
     both[0:width, :] = latent
@@ -271,12 +306,15 @@
         weights = first_t.at[r]
         now = both[0:width, :]
         received[...] = dot(weights[:, width : 2 * width], now)
-        near_left[:, 0:particles] = dot(weights[:, 2 * width :], now).astype(BF16)
-        near_left[:, particles : particles + width] = weights[:, 0:width]
+        own_left[...] = dot(weights[:, 2 * width :], now).astype(BF16)
+        near_left[:, 0:width] = weights[:, 0:width]
 
     for r in range(rounds):
         send(slots, *path(r))
         if r == 0:
+            for n in range(19):
+                if n not in urgent:
+                    fetches[n].wait()
             base[...] = edge_features(off_ref, enc_edge_w1, square, feature).astype(BF16)
             enc_second = dot_nt(center_of, enc_edge_w2[...]).astype(BF16)
             prepare_indices(slots, index_ref, local_code, ghost_code, row_code, ghosts)
@@ -287,15 +325,15 @@
                 hidden[k] = jnp.maximum(dot(left, feature[...]), 0.0).astype(BF16)
                 return carry
 
-            lax.fori_loop(0, pair_slots, first_edge, 0, unroll=4)
+            lax.fori_loop(0, pair_slots, first_edge, 0, unroll=pair_slots)
 
             def second_edge(k, carry):
                 fresh = normed(dot(enc_second, hidden[k])).astype(BF16)
-                near[k, particles : particles + width, :] = fresh
-                fill_pair_hot(k, local_code, ghost_code, row_code, near, far, width, ghosts)
+                near[k, 0:width, :] = fresh
+                fill_pair_hot(k, local_code, ghost_code, row_code, own, near, far, width)
                 return carry
 
-            lax.fori_loop(0, pair_slots, second_edge, 0, unroll=4)
+            lax.fori_loop(0, pair_slots, second_edge, 0, unroll=pair_slots)
             turn_weights(0)
             square[0:rounds, :] = edge_gain[...]
             square[rounds : 2 * rounds, :] = node_gain[...]
@@ -303,43 +341,47 @@
             for g in range(2 * rounds):
                 gains[g] = jnp.broadcast_to(columns[:, g : g + 1], (width, width))
         local_part(r)
-        land(slots, [0], *path(r))
-        first_ghosts = inbox[r, 0]
-        near_left[:, particles + width :] = dot_nt(first_t[r, :, 2 * width :], first_ghosts).astype(BF16)
-
-        def early(k, carry):
-            partial[k] = dot(near_left[...], near[k]) + received[...]
+
+        def local(k, carry):
+            partial[k] = dot(own_left[...], own[k]) + received[...]
             return carry
 
-        lax.fori_loop(0, pair_slots, early, 0, unroll=4)
+        lax.fori_loop(0, pair_slots, local, 0, unroll=pair_slots)
         if r + 1 < rounds:
             turn_weights(r + 1)
-        land(slots, range(1, len(slots)), *path(r))
-        late_ghosts = inbox[r, 1:].reshape(-1, width)
-        far_left[...] = dot_nt(first_t[r, :, 2 * width :], late_ghosts).astype(BF16)
-
-        def late(k, carry):
-            hidden[k] = jnp.maximum(partial[k] + dot(far_left[...], far[k]), 0.0).astype(BF16)
+        land(slots, range(faces), *path(r))
+        near_left[:, width:] = dot_nt(
+            first_t[r, :, 2 * width :], inbox[r, 0:faces].reshape(-1, width)
+        ).astype(BF16)
+
+        def early(k, carry):
+            partial[k] = partial[k] + dot(near_left[...], near[k])
             return carry
 
-        lax.fori_loop(0, pair_slots, late, 0, unroll=4)
-
-        def second(k, carry):
-            center = dot(second_c[r], hidden[k])
-            partial[k] = center
-            scale = inverse_spread(jnp.sum(center * center, axis=0, keepdims=True), width)
-            squares[k] = jnp.broadcast_to(jnp.where(k < count_ref[...], scale, 0.0), squares.shape[1:])
-            return carry
-
-        lax.fori_loop(0, pair_slots, second, 0, unroll=4)
-
+        lax.fori_loop(0, pair_slots, early, 0, unroll=pair_slots)
+        land(slots, range(faces, len(slots)), *path(r))
+        far_left[...] = dot_nt(
+            first_t[r, :, 2 * width :], inbox[r, faces:].reshape(-1, width)
+        ).astype(BF16)
         edge_column = jnp.concatenate([gains[r]] * (particles // width), axis=1)
         node_column = jnp.concatenate([gains[rounds + r]] * (particles // width), axis=1)
-        for f in range(0, width, 8):
-            total = partial[0, f : f + 8, :] * squares[0]
-            for k in range(1, pair_slots):
-                total = total + partial[k, f : f + 8, :] * squares[k]
-            received[f : f + 8, :] = total
+        group = 4
+        for start in range(0, pair_slots, group):
+            members = range(start, start + group)
+            for k in members:
+                hidden[k] = jnp.maximum(partial[k] + dot(far_left[...], far[k]), 0.0).astype(BF16)
+            for k in members:
+                center = dot(second_c[r], hidden[k])
+                partial[k] = center
+                scale = inverse_spread(jnp.sum(center * center, axis=0, keepdims=True), width)
+                scale = jnp.where(k < count_ref[...], scale, 0.0)
+                squares[k] = jnp.broadcast_to(scale, squares.shape[1:])
+            for f in range(0, width, 8):
+                total = functools.reduce(
+                    jnp.add, [partial[k, f : f + 8, :] * squares[k] for k in members]
+                )
+                received[f : f + 8, :] = total + received[f : f + 8, :] if start else total
+
         both[width : 2 * width, :] = (received[...] * edge_column).astype(BF16)
         middle = jnp.maximum(dot(node_t[r], both[...]), 0.0).astype(BF16)
         update = normed(dot(node_c[r], middle)) * node_column
@@ -391,9 +433,10 @@
     ghosts = send_rows.shape[1]
     state_rows = kinematics.shape[0]
     rounds = edge_w1.shape[0]
-    slot_count = len(Slots([lax.axis_size(axis) for axis in AXES]))
-    near_rows = particles + width + ghosts
-    far_rows = (slot_count - 1) * ghosts
+    slots = Slots([lax.axis_size(axis) for axis in AXES])
+    count = len(slots)
+    near_rows = width + slots.faces * ghosts
+    far_rows = (count - slots.faces) * ghosts
     operands = (
         kinematics, pair_offsets, pair_index, neighbour_count.reshape(1, particles), send_rows.T,
         migrate_dir.reshape(1, particles), migrate_slot.reshape(1, particles), enc_node_w1,
@@ -401,51 +444,53 @@
         node_gain, dec_w1, dec_w2,
     )
     vmem = pl.BlockSpec(memory_space=pltpu.VMEM)
-    return tuple(
-        pl.pallas_call(
-            step_kernel,
-            name="step",
-            in_specs=[vmem] * len(operands),
-            out_specs=[vmem, vmem],
-            out_shape=[
-                jax.ShapeDtypeStruct((state_rows, particles), F32),
-                jax.ShapeDtypeStruct((state_rows, 27 * MIG), F32),
-            ],
-            scratch_shapes=[
-                pltpu.VMEM((rounds, slot_count, ghosts, width), BF16),
-                pltpu.VMEM((rounds, slot_count, ghosts, width), BF16),
-                pltpu.VMEM((27, MIG, width), F32),
-                pltpu.VMEM((27, MIG, width), F32),
-                pltpu.SemaphoreType.DMA((rounds + 1, slot_count)),
-                pltpu.SemaphoreType.DMA((rounds + 1, slot_count)),
-                pltpu.VMEM((width, width), F32),
-                pltpu.VMEM((width, particles), F32),
-                pltpu.VMEM((12 * pair_slots, particles), BF16),
-                pltpu.VMEM((width, 12 * pair_slots), BF16),
-                pltpu.VMEM((pair_slots, particles), F32),
-                pltpu.VMEM((pair_slots, particles), F32),
-                pltpu.VMEM((particles + slot_count * ghosts, particles), BF16),
-                pltpu.VMEM((slot_count * ghosts, particles), BF16),
-                pltpu.VMEM((pair_slots, near_rows, particles), BF16),
-                pltpu.VMEM((pair_slots, far_rows, particles), BF16),
-                pltpu.VMEM((pair_slots, width, particles), BF16),
-                pltpu.VMEM((pair_slots, width, particles), F32),
-                pltpu.VMEM((pair_slots, 8, particles), F32),
-                pltpu.VMEM((width, near_rows), BF16),
-                pltpu.VMEM((width, far_rows), BF16),
-                pltpu.VMEM((width, particles), F32),
-                pltpu.VMEM((rounds, width, 3 * width), BF16),
-                pltpu.VMEM((rounds, width, width), BF16),
-                pltpu.VMEM((rounds, width, 2 * width), BF16),
-                pltpu.VMEM((rounds, width, width), BF16),
-                pltpu.VMEM((2 * rounds, width, width), F32),
-                pltpu.VMEM((2 * width, particles), BF16),
-                pltpu.VMEM((32, particles), F32),
-                pltpu.VMEM((width, width), F32),
-            ],
-            compiler_params=pltpu.CompilerParams(collective_id=0, has_side_effects=True),
-        )(*operands)
-    )
+    anywhere = pl.BlockSpec(memory_space=pl.ANY)
+    shapes = [(state_rows, particles), (state_rows, 27 * MIG)]
+    found = pl.pallas_call(
+        functools.partial(step_kernel, slots),
+        name="step",
+        in_specs=[anywhere] * len(operands),
+        out_specs=[vmem, vmem],
+        out_shape=[pltpu.VMEM(shape, F32) for shape in shapes],
+        scratch_shapes=[pltpu.VMEM(operand.shape, operand.dtype) for operand in operands]
+        + [
+            pltpu.SemaphoreType.DMA((len(operands),)),
+            pltpu.VMEM((rounds, count, ghosts, width), BF16),
+            pltpu.VMEM((rounds, count, ghosts, width), BF16),
+            pltpu.VMEM((27, MIG, width), F32),
+            pltpu.VMEM((27, MIG, width), F32),
+            pltpu.SemaphoreType.DMA((rounds + 1, count)),
+            pltpu.SemaphoreType.DMA((rounds + 1, count)),
+            pltpu.VMEM((width, width), F32),
+            pltpu.VMEM((width, particles), F32),
+            pltpu.VMEM((12 * pair_slots, particles), BF16),
+            pltpu.VMEM((width, 12 * pair_slots), BF16),
+            pltpu.VMEM((pair_slots, particles), F32),
+            pltpu.VMEM((pair_slots, particles), F32),
+            pltpu.VMEM((particles + count * ghosts, particles), BF16),
+            pltpu.VMEM((count * ghosts, particles), BF16),
+            pltpu.VMEM((pair_slots, particles, particles), BF16),
+            pltpu.VMEM((pair_slots, near_rows, particles), BF16),
+            pltpu.VMEM((pair_slots, far_rows, particles), BF16),
+            pltpu.VMEM((pair_slots, width, particles), BF16),
+            pltpu.VMEM((pair_slots, width, particles), F32),
+            pltpu.VMEM((pair_slots, 8, particles), F32),
+            pltpu.VMEM((width, particles), BF16),
+            pltpu.VMEM((width, near_rows), BF16),
+            pltpu.VMEM((width, far_rows), BF16),
+            pltpu.VMEM((width, particles), F32),
+            pltpu.VMEM((rounds, width, 3 * width), BF16),
+            pltpu.VMEM((rounds, width, width), BF16),
+            pltpu.VMEM((rounds, width, 2 * width), BF16),
+            pltpu.VMEM((rounds, width, width), BF16),
+            pltpu.VMEM((2 * rounds, width, width), F32),
+            pltpu.VMEM((2 * width, particles), BF16),
+            pltpu.VMEM((32, particles), F32),
+            pltpu.VMEM((width, width), F32),
+        ],
+        compiler_params=pltpu.CompilerParams(collective_id=0, has_side_effects=True),
+    )(*operands)
+    return tuple(found)
 
 
 def solution(mesh):

time: 35.6 us -> 28.7 us (0.81)
  Pallas kernels: 32.8 us -> 26.6 us
  local copies, waits for them, and re-layouts: 1.96 us -> 1.21 us
    pallas_call x1, Pallas kernels: 32.8 us -> 26.6 us  [on_device(): pl.pallas_call(functools.partial(step_kernel, slots), name='step', in_spe...]
    unnamed x4 -> x2, local copies, waits for them, and re-layouts: 1.96 us -> 1.21 us
where the time goes in v2:
time: 28.7 us; the launch traced here: 28.4 us
  Pallas kernels  26.6 us (93%)
  local copies, waits for them, and re-layouts  1.21 us (4%)
  between operations  0.65 us (2%)
    pallas_call x1, Pallas kernels, on_device(): pl.pallas_call(functools.partial(step_kernel, slots), name='step', in_spe...  26.6 us
    unnamed x2, local copies, waits for them, and re-layouts  1.21 us

profile of v2, /device:TPU:1, one launch (start us, length us, event | category | flops | bytes accessed | tf_op | source)
XLA Modules:
  0.0 28.4 jit_solution(13141444640935105502)
XLA Ops:
  0.6 26.6 %step.1 = (f32[18,256]{1,0:T(8,128)S(1)}, f32[18,108]{1,0:T(8,128)S(1)}) custom-call(f32[18,256]{1,0:T(8,128)} %refs_0_.1, f32[3,16,256]{2,1,0:T(8,128)} %refs_1_.1, s32[16,256]{1,0:T(8,128)} %refs_2_.1, s32[1,256]{1,0:T(1,128)} %bitcast.5, s32[16,27]{1,0:T(8,128)} %bitcast.4, s32[1,256]{1,0:T(1,128)} %bitcast.6, s32[1,256]{1,0:T(1,128)} %bitcast.7, ...), custom_call_target="tpu_custom_call" | custom-call | tf_op jit(solution)/shard_map/step/pallas_call | solution.py:449
  27.2 0.6 %copy.23 = f32[18,256]{1,0:T(8,128)} copy(f32[18,256]{1,0:T(8,128)S(1)} %get-tuple-element.2) | data formatting | bytes 36864
  27.8 0.6 %copy.24 = f32[18,108]{1,0:T(8,128)} copy(f32[18,108]{1,0:T(8,128)S(1)} %get-tuple-element.3) | data formatting | bytes 15552

commit v3 on v2

--- a/solution.py
+++ b/solution.py
@@ -365,23 +365,19 @@
         ).astype(BF16)
         edge_column = jnp.concatenate([gains[r]] * (particles // width), axis=1)
         node_column = jnp.concatenate([gains[rounds + r]] * (particles // width), axis=1)
-        group = 4
-        for start in range(0, pair_slots, group):
-            members = range(start, start + group)
-            for k in members:
-                hidden[k] = jnp.maximum(partial[k] + dot(far_left[...], far[k]), 0.0).astype(BF16)
-            for k in members:
-                center = dot(second_c[r], hidden[k])
-                partial[k] = center
-                scale = inverse_spread(jnp.sum(center * center, axis=0, keepdims=True), width)
-                scale = jnp.where(k < count_ref[...], scale, 0.0)
-                squares[k] = jnp.broadcast_to(scale, squares.shape[1:])
-            for f in range(0, width, 8):
-                total = functools.reduce(
-                    jnp.add, [partial[k, f : f + 8, :] * squares[k] for k in members]
-                )
-                received[f : f + 8, :] = total + received[f : f + 8, :] if start else total
-
+        for k in range(pair_slots):
+            hidden[k] = jnp.maximum(partial[k] + dot(far_left[...], far[k]), 0.0).astype(BF16)
+        for k in range(pair_slots):
+            center = dot(second_c[r], hidden[k])
+            partial[k] = center
+            scale = inverse_spread(jnp.sum(center * center, axis=0, keepdims=True), width)
+            scale = jnp.where(k < count_ref[...], scale, 0.0)
+            squares[k] = jnp.broadcast_to(scale, squares.shape[1:])
+        for f in range(0, width, 8):
+            total = partial[0, f : f + 8, :] * squares[0]
+            for k in range(1, pair_slots):
+                total = total + partial[k, f : f + 8, :] * squares[k]
+            received[f : f + 8, :] = total
         both[width : 2 * width, :] = (received[...] * edge_column).astype(BF16)
         middle = jnp.maximum(dot(node_t[r], both[...]), 0.0).astype(BF16)
         update = normed(dot(node_c[r], middle)) * node_column
@@ -421,6 +417,17 @@
     for q in range(27):
         rows[MIG * q : MIG * (q + 1), :] = landed[q]
     arrived_ref[...] = rows[...].T[0:state_rows, 0 : 27 * MIG]
+
+
+def deliver(stayed_ref, arrived_ref, stayed_out, arrived_out, sems):
+    copies = [
+        pltpu.make_async_copy(stayed_ref, stayed_out, sems.at[0]),
+        pltpu.make_async_copy(arrived_ref, arrived_out, sems.at[1]),
+    ]
+    for copy in copies:
+        copy.start()
+    for copy in copies:
+        copy.wait()
 
 
 def on_device(
@@ -490,7 +497,18 @@
         ],
         compiler_params=pltpu.CompilerParams(collective_id=0, has_side_effects=True),
     )(*operands)
-    return tuple(found)
+    found = [pltpu.with_memory_space_constraint(x, pltpu.VMEM) for x in found]
+    return tuple(
+        pl.pallas_call(
+            deliver,
+            name="deliver",
+            in_specs=[vmem] * 2,
+            out_specs=[anywhere] * 2,
+            out_shape=[jax.ShapeDtypeStruct(shape, F32) for shape in shapes],
+            scratch_shapes=[pltpu.SemaphoreType.DMA((2,))],
+            compiler_params=pltpu.CompilerParams(vmem_limit_bytes=1 << 20),
+        )(*found)
+    )
 
 
 def solution(mesh):

time: 28.7 us -> 26.6 us (0.927)
  local copies, waits for them, and re-layouts: 1.21 us -> 0 us
  Pallas kernels: 26.6 us -> 25.7 us
    pallas_call x1, Pallas kernels: 26.6 us -> 25.1 us  [on_device(): pl.pallas_call(functools.partial(step_kernel, slots), name='step', in_spe...]
    unnamed x2 -> x0, local copies, waits for them, and re-layouts: 1.21 us -> none
    pallas_call x0 -> x1, Pallas kernels: none -> 0.63 us  [on_device(): pl.pallas_call(deliver, name='deliver', in_specs=[vmem] * 2, out_specs=[a...]
where the time goes in v3:
time: 26.6 us; the launch traced here: 26.4 us
  Pallas kernels  25.7 us (97%)
  between operations  0.65 us (2%)
    pallas_call x1, Pallas kernels, on_device(): pl.pallas_call(functools.partial(step_kernel, slots), name='step', in_spe...  25.1 us
    pallas_call x1, Pallas kernels, on_device(): pl.pallas_call(deliver, name='deliver', in_specs=[vmem] * 2, out_specs=[a...  0.63 us

profile of v3, /device:TPU:1, one launch (start us, length us, event | category | flops | bytes accessed | tf_op | source)
XLA Modules:
  0.0 26.4 jit_solution(2868070964931195174)
XLA Ops:
  0.6 25.1 %step.1 = (f32[18,256]{1,0:T(8,128)S(1)}, f32[18,108]{1,0:T(8,128)S(1)}) custom-call(f32[18,256]{1,0:T(8,128)} %refs_0_.1, f32[3,16,256]{2,1,0:T(8,128)} %refs_1_.1, s32[16,256]{1,0:T(8,128)} %refs_2_.1, s32[1,256]{1,0:T(1,128)} %bitcast.5, s32[16,27]{1,0:T(8,128)} %bitcast.4, s32[1,256]{1,0:T(1,128)} %bitcast.6, s32[1,256]{1,0:T(1,128)} %bitcast.7, ...), custom_call_target="tpu_custom_call" | custom-call | tf_op jit(solution)/shard_map/step/pallas_call | solution.py:456
  25.7 0.6 %deliver.1 = (f32[18,256]{1,0:T(8,128)}, f32[18,108]{1,0:T(8,128)}) custom-call(f32[18,256]{1,0:T(8,128)S(1)} %get-tuple-element.4.stayed_ref, f32[18,108]{1,0:T(8,128)S(1)} %get-tuple-element.5.arrived_ref), custom_call_target="tpu_custom_call" | custom-call | tf_op jit(solution)/shard_map/deliver/pallas_call | solution.py:502

commit v4 on v3

--- a/solution.py
+++ b/solution.py
@@ -117,7 +117,7 @@
 
 def enter(slots):
     barrier = pltpu.get_barrier_semaphore()
-    for n in range(len(slots)):
+    for n in reversed(range(len(slots))):
         there, inside = slots.peer(n)
         guarded(inside, lambda: pl.semaphore_signal(barrier, inc=1, device_id=there, device_id_type=MESH))
     peers = 1
@@ -262,7 +262,8 @@
     (
         copy_sems, outbox, inbox, leaving, landed, send_sems, recv_sems, square, wide, feature, base,
         local_code, ghost_code, row_code, send_hot, own, near, far, hidden, partial, squares, own_left,
-        near_left, far_left, received, first_t, second_c, node_t, node_c, gains, both, state, rows,
+        near_left, far_left, received, first_t, second_c, node_t, node_c, gains, both, state, rows, dec_t,
+        picker,
     ) = scratch[19:]
     width = enc_node_w2.shape[1]
     state_rows, particles = kin_ref.shape
@@ -349,6 +350,15 @@
         lax.fori_loop(0, pair_slots, local, 0, unroll=pair_slots)
         if r + 1 < rounds:
             turn_weights(r + 1)
+        else:
+            reading = dec_w2[...]
+            wide[...] = jnp.zeros_like(wide)
+            wide[0:3, 0:width] = reading
+            wide[8:11, 0:width] = reading - head(reading)
+            wide[16:19, 0:width] = reading - head(reading) - head(reading - head(reading))
+            dec_t[...] = dot_nt(unit, dec_w1[...]).astype(BF16)
+            target = jnp.where(dir_ref[...] == 13, -1, dir_ref[...] * MIG + slot_ref[...])
+            picker[...] = jnp.where(iota(picker.shape, 0) == target, 1.0, 0.0).astype(BF16)
         land(slots, range(faces), *path(r))
         near_left[:, width:] = dot_nt(
             first_t[r, :, 2 * width :], inbox[r, 0:faces].reshape(-1, width)
@@ -373,11 +383,15 @@
             scale = inverse_spread(jnp.sum(center * center, axis=0, keepdims=True), width)
             scale = jnp.where(k < count_ref[...], scale, 0.0)
             squares[k] = jnp.broadcast_to(scale, squares.shape[1:])
-        for f in range(0, width, 8):
-            total = partial[0, f : f + 8, :] * squares[0]
-            for k in range(1, pair_slots):
-                total = total + partial[k, f : f + 8, :] * squares[k]
-            received[f : f + 8, :] = total
+        half = pair_slots // 2
+        for start in (0, half):
+            members = range(start, start + half)
+            scales = [squares[k] for k in members]
+            for f in range(0, width, 8):
+                total = functools.reduce(
+                    jnp.add, [partial[k, f : f + 8, :] * scale for k, scale in zip(members, scales)]
+                )
+                received[f : f + 8, :] = total + received[f : f + 8, :] if start else total
         both[width : 2 * width, :] = (received[...] * edge_column).astype(BF16)
         middle = jnp.maximum(dot(node_t[r], both[...]), 0.0).astype(BF16)
         update = normed(dot(node_c[r], middle)) * node_column
@@ -386,28 +400,22 @@
         if r + 1 < rounds:
             outbox[r + 1] = dot_nt(send_hot[...], latent).astype(BF16).reshape(outbox.shape[1:])
 
-    reading = dec_w2[...]
-    wide[...] = jnp.zeros_like(wide)
-    wide[0:3, 0:width] = reading
-    wide[8:11, 0:width] = reading - head(reading)
-    wide[16:19, 0:width] = reading - head(reading) - head(reading - head(reading))
-    readout = wide[0:32, 0:width].astype(BF16)
-    decoded = jnp.maximum(dot(dot_nt(unit, dec_w1[...]).astype(BF16), latent), 0.0).astype(BF16)
-    parts = dot(readout, decoded)
+    decoded = jnp.maximum(dot(dec_t[...], latent), 0.0).astype(BF16)
+    parts = dot(wide[0:32, 0:width].astype(BF16), decoded)
     velocity = kin_ref[state_rows - 3 :, :] + (parts[0:3, :] + (parts[8:11, :] + parts[16:19, :]))
     state[...] = jnp.zeros_like(state)
     state[0:3, :] = kin_ref[0:3, :] + velocity
     state[3 : state_rows - 3, :] = kin_ref[6:, :]
     state[state_rows - 3 : state_rows, :] = velocity
     staying = dir_ref[...] == 13
-    target = jnp.where(staying, -1, dir_ref[...] * MIG + slot_ref[...])
-    picker = jnp.where(iota((rows.shape[0], particles), 0) == target, 1.0, 0.0).astype(BF16)
     whole = state[...]
     high = whole.astype(BF16)
     rest = whole - high.astype(F32)
     middle = rest.astype(BF16)
     low = (rest - middle.astype(F32)).astype(BF16)
-    rows[:, 0 : state.shape[0]] = dot_nt(picker, high) + dot_nt(picker, middle) + dot_nt(picker, low)
+    rows[:, 0 : state.shape[0]] = (
+        dot_nt(picker[...], high) + dot_nt(picker[...], middle) + dot_nt(picker[...], low)
+    )
     for q in range(27):
         leaving[q] = rows[MIG * q : MIG * (q + 1), :]
     migration = (leaving, landed, send_sems.at[rounds], recv_sems.at[rounds])
@@ -494,6 +502,8 @@
             pltpu.VMEM((2 * width, particles), BF16),
             pltpu.VMEM((32, particles), F32),
             pltpu.VMEM((width, width), F32),
+            pltpu.VMEM((width, width), BF16),
+            pltpu.VMEM((width, particles), BF16),
         ],
         compiler_params=pltpu.CompilerParams(collective_id=0, has_side_effects=True),
     )(*operands)

time: 26.6 us -> 26.3 us (0.989)
  Pallas kernels: 25.7 us -> 25.4 us
    pallas_call x1, Pallas kernels: 25.1 us -> 24.8 us  [on_device(): pl.pallas_call(functools.partial(step_kernel, slots), name='step', in_spe...]
where the time goes in v4:
time: 26.3 us; the launch traced here: 26.1 us
  Pallas kernels  25.4 us (97%)
  between operations  0.65 us (2%)
    pallas_call x1, Pallas kernels, on_device(): pl.pallas_call(functools.partial(step_kernel, slots), name='step', in_spe...  24.8 us
    pallas_call x1, Pallas kernels, on_device(): pl.pallas_call(deliver, name='deliver', in_specs=[vmem] * 2, out_specs=[a...  0.63 us

profile of v4, /device:TPU:1, one launch (start us, length us, event | category | flops | bytes accessed | tf_op | source)
XLA Modules:
  0.0 26.1 jit_solution(4962365752523710704)
XLA Ops:
  0.6 24.8 %step.1 = (f32[18,256]{1,0:T(8,128)S(1)}, f32[18,108]{1,0:T(8,128)S(1)}) custom-call(f32[18,256]{1,0:T(8,128)} %refs_0_.1, f32[3,16,256]{2,1,0:T(8,128)} %refs_1_.1, s32[16,256]{1,0:T(8,128)} %refs_2_.1, s32[1,256]{1,0:T(1,128)} %bitcast.5, s32[16,27]{1,0:T(8,128)} %bitcast.4, s32[1,256]{1,0:T(1,128)} %bitcast.6, s32[1,256]{1,0:T(1,128)} %bitcast.7, ...), custom_call_target="tpu_custom_call" | custom-call | tf_op jit(solution)/shard_map/step/pallas_call | solution.py:464
  25.4 0.6 %deliver.1 = (f32[18,256]{1,0:T(8,128)}, f32[18,108]{1,0:T(8,128)}) custom-call(f32[18,256]{1,0:T(8,128)S(1)} %get-tuple-element.4.stayed_ref, f32[18,108]{1,0:T(8,128)S(1)} %get-tuple-element.5.arrived_ref), custom_call_target="tpu_custom_call" | custom-call | tf_op jit(solution)/shard_map/deliver/pallas_call | solution.py:512
